TPU v7x, 128 devices: a whole 4x4x4 slice. The times are simulated.
128 devices in a mesh: zg: 2 (over x_lo), xy: 64 (over x_hi, y, z, core).
Axes of the slice: x: 4 (x_hi: 2, x_lo: 2; x = x_hi * 2 + x_lo), y: 4, z: 4, core: 2. Of those that a mesh axis runs over, the one named last changes fastest.
Arguments:
- charges: float32 [262144], P(('zg', 'xy')), may hold values from -12 to 12
- cells: int32 [8, 262144], P(None, ('zg', 'xy')), may hold values from 0 to 786431
- splines: float32 [8, 262144], P(None, ('zg', 'xy')), may hold values from 0.05 to 1
- counts: int32 [128], P(('zg', 'xy')), may hold values from 1024 to 2048, as said below
- green: bfloat16 [512, 4, 384, 384], P(('zg', 'xy')), may hold values from -0.3125 to 0.3125
Outputs:
- potential: float32 [384, 512, 512], P(('zg', 'xy'))
Inputs may be any that keep to these rules, and one draw needn't show every extreme that they name: `counts`: some device has all 2048 slots live in every draw.
All inputs are finite; a program needn't handle non-finite values.
Results may differ from a plain program's by a relative error of at most 0.0041.
Values may be sent and summed in bfloat16 or wider, within the bound.
No kernel may reach another device: no remote copies, remote signals or barrier semaphores. Data moves between devices by JAX's collectives and lax.ppermute only.
A program may use at most 64 MiB of HBM per device.

v0:
```python
import math
import jax
import jax.numpy as jnp
from jax import lax
from jax.sharding import PartitionSpec as P

NX = 512
NY = 512
NZ = 384
KYB = 4


def tables(length):
    index = jnp.arange(length, dtype=jnp.int32)
    product = index[:, None] * index[None, :] % length
    angle = product.astype(jnp.float32) * (2.0 * math.pi / length)
    return (jnp.cos(angle), jnp.sin(angle))


def shards(charges, cells, splines, counts, green):
    groups = lax.axis_size("zg")
    rows = lax.axis_size("xy")
    slab = NZ // (groups * rows)
    slots = charges.shape[0]
    live = (jnp.arange(slots, dtype=jnp.int32) < counts[0]).astype(jnp.float32)
    values = splines * (charges * live)[None, :]
    density = (
        jnp.zeros((slab * NX * NY,), jnp.float32).at[cells.reshape(-1)].add(values.reshape(-1))
    )
    density = density.reshape(slab, NX, NY)
    cos_y, sin_y = tables(NY)
    cos_x, sin_x = tables(NX)
    scale = 1.0 / math.sqrt(NX * NY)
    forward_y = jnp.stack([cos_y, -sin_y], axis=1)
    along = jnp.einsum("zxy,yev->zxev", density, forward_y, precision=lax.Precision.HIGHEST)
    forward_x = jnp.stack(
        [jnp.stack([cos_x, sin_x], axis=1), jnp.stack([-sin_x, cos_x], axis=1)], axis=0
    )
    spectrum = (
        jnp.einsum("cuex,zxev->zcuv", forward_x, along, precision=lax.Precision.HIGHEST) * scale
    ).astype(jnp.bfloat16)
    pencil = lax.all_to_all(spectrum, ("zg", "xy"), split_axis=2, concat_axis=0, tiled=True)
    depth, parts, waves, width = pencil.shape
    blocks = pencil.reshape(depth, parts, waves, KYB, width // KYB)
    mixed = jnp.einsum("abzw,wcabj->zcabj", green, blocks, preferred_element_type=jnp.float32)
    returned = lax.all_to_all(
        mixed.reshape(depth, parts, waves, width).astype(jnp.bfloat16),
        ("zg", "xy"),
        split_axis=0,
        concat_axis=2,
        tiled=True,
    )
    inverse_x = jnp.stack(
        [jnp.stack([cos_x, -sin_x], axis=1), jnp.stack([sin_x, cos_x], axis=1)], axis=1
    )
    upper_x = inverse_x.astype(jnp.bfloat16)
    lower_x = (inverse_x - upper_x.astype(jnp.float32)).astype(jnp.bfloat16)
    middle = jnp.einsum("xceu,zeuv->zxcv", upper_x, returned, preferred_element_type=jnp.float32)
    middle = middle + jnp.einsum(
        "xceu,zeuv->zxcv", lower_x, returned, preferred_element_type=jnp.float32
    )
    inverse_y = jnp.stack([cos_y, -sin_y], axis=0)
    potential = (
        jnp.einsum("zxcv,cvy->zxy", middle, inverse_y, precision=lax.Precision.HIGHEST) * scale
    )
    return potential


def solution(mesh):
    in_specs = (
        P(("zg", "xy")),
        P(None, ("zg", "xy")),
        P(None, ("zg", "xy")),
        P(("zg", "xy")),
        P(("zg", "xy"), None, None, None),
    )
    out_specs = P(("zg", "xy"), None, None)
    return jax.shard_map(shards, mesh=mesh, in_specs=in_specs, out_specs=out_specs, check_vma=False)
```

profile of v0, /device:TPU:1, one launch (start us, length us, event | category | flops | bytes accessed | tf_op | source)
XLA Modules:
  0.0 296.6 jit_solution(15891612420639336365)
XLA Ops:
  0.0 5.0 %fusion.51 = (f32[512,1,512]{2,0,1:T(8,128)}, f32[512,1,512]{2,0,1:T(8,128)}) fusion(), kind=kLoop, calls=%fused_computation.61 | loop fusion | flops 3670016 | bytes 2097152 | tf_op jit(solution)/shard_map/sin | solution.py:17
  5.0 4.6 %fusion.53 = f32[512,1,512]{2,0,1:T(8,128)} fusion(), kind=kLoop, calls=%fused_computation.63 | loop fusion | flops 3932160 | bytes 1048576 | tf_op jit(solution)/shard_map/neg | solution.py:34
  10.2 0.0 copy-done.9
  10.3 0.0 copy-done.7
  10.3 0.0 copy-done.8
  10.3 0.1 copy.48
  10.4 0.1 compare_select_fusion
  10.5 86.7 %scatter_custom_fusion = f32[786432]{0:T(1024)S(1)} fusion(s32[16384]{0:T(1024)S(1)} %bitcast.109, f32[16384]{0:T(1024)S(1)} %bitcast.108, f32[]{:T(128)} %constant.24.clone.1), kind=kCustom, calls=%fused_computation.45 | custom fusion | flops 16384 | bytes 3145732 | tf_op jit(solution)/shard_map/scatter-add | solution.py:28
  97.2 2.3 reshape.202
  99.5 6.1 %fusion.35 = (f32[512,1,2,512]{3,0,2,1:T(8,128)}, f32[1,512,2,512]{3,1,2,0:T(8,128)S(1)}, f32[1,512,2,512]{3,1,2,0:T(8,128)S(1)}, f32[512,1,2,512]{3,0,2,1:T(8,128)}) fusion(f32[512,1,512]{2,0,1:T(8,128)} %fusion.53, f32[512,1,512]{2,0,1:T(8,128)} %get-tuple-element.12, f32[512,1,512]{2,0,1:T(8,128)} %get-tuple-element.11), kind=kLoop, calls=%fused_computation.38 | loop fusion | flops 2097152 | bytes 11534336 | tf_op jit(solution)/shard_map/stack | solution.py:53
  105.6 0.0 copy-done
  105.6 10.1 %fusion.12 = f32[3,512,2,512]{1,3,2,0:T(8,128)S(1)} fusion(f32[3,512,512,1]{2,1,0,3:T(8,128)S(1)} %copy-done, f32[512,1,512]{2,0,1:T(8,128)S(1)} %copy-done.1, f32[512,1,512]{2,0,1:T(8,128)S(1)} %copy-done.2), kind=kOutput, calls=%fused_computation.19 | convolution fusion | flops 9664200704 | bytes 11534336 | tf_op jit(solution)/shard_map/zxy,yev->zxev/dot_general | solution.py:35
  115.8 22.1 %fusion.11 = bf16[3,2,512,512]{2,3,1,0:T(8,128)(2,1)} fusion(f32[1,512,2,512]{3,1,2,0:T(8,128)S(1)} %get-tuple-element.6, f32[1,512,2,512]{3,1,2,0:T(8,128)S(1)} %get-tuple-element.9, f32[3,512,2,512]{1,3,2,0:T(8,128)S(1)} %fusion.12), kind=kOutput, calls=%fused_computation.17 | convolution fusion | flops 19331547136 | bytes 13631488 | tf_op jit(solution)/shard_map/cuex,zxev->zcuv/dot_general | solution.py:40
  137.8 7.3 %copy.22 = bf16[3,2,512,512]{3,1,0,2:T(2,128)(2,1)S(1)} copy(bf16[3,2,512,512]{2,3,1,0:T(8,128)(2,1)} %fusion.11) | data formatting | bytes 6291456 | tf_op jit(solution)/shard_map/convert_element_type | solution.py:41
  145.2 53.2 %all_to_all.33 = bf16[3,2,512,512]{3,1,0,2:T(2,128)(2,1)S(1)} all-to-all(bf16[3,2,512,512]{3,1,0,2:T(2,128)(2,1)S(1)} %copy.22), channel_id=1, replica_groups=mesh['zg'=2,'xy'=64] {'zg','xy'}, dimensions={2} | all-to-all | bytes 6291456 | tf_op jit(solution)/shard_map/all_to_all | solution.py:42
  198.4 3.3 %copy.24 = bf16[128,3,2,4,512]{4,3,2,1,0:T(4,128)(2,1)} copy(bf16[128,3,2,4,512]{4,2,1,3,0:T(2,128)(2,1)S(1)} %bitcast.103) | data formatting | bytes 6291456 | tf_op jit(solution)/shard_map/all_to_all | solution.py:42
  201.6 4.0 %reshape.193 = bf16[384,2,4,4,128]{4,3,2,1,0:T(4,128)(2,1)S(1)} reshape(bf16[128,3,2,4,512]{4,3,2,1,0:T(4,128)(2,1)} %copy.24) | data formatting | bytes 6291456 | tf_op jit(solution)/shard_map/reshape | solution.py:44
  205.7 5.4 %convert_bitcast_fusion = bf16[384,2,4,4,128]{0,4,1,3,2:T(8,128)(2,1)S(1)} fusion(bf16[4,4,384,384]{3,2,1,0:T(8,128)(2,1)} %param.9, bf16[384,2,4,4,128]{4,3,2,1,0:T(4,128)(2,1)S(1)} %reshape.193), kind=kOutput, calls=%fused_computation.22 | convolution fusion | flops 1209532416 | bytes 11010048 | tf_op jit(solution)/shard_map/abzw,wcabj->zcabj/dot_general | solution.py:45
  211.1 0.4 copy.26
  211.5 4.4 %copy.27 = bf16[384,2,4,512]{3,2,1,0:T(4,128)(2,1)} copy(bf16[384,2,4,512]{0,3,2,1:T(8,128)(2,1)S(1)} %bitcast.104) | data formatting | bytes 6291456 | tf_op jit(solution)/shard_map/convert_element_type | solution.py:47
  215.8 4.8 %all-to-all-start.1 = ((bf16[384,2,4,512]{3,2,1,0:T(4,128)(2,1)}), bf16[384,2,4,512]{3,2,1,0:T(4,128)(2,1)S(1)}, u32[]{:S(2)}, u32[]{:S(2)}) async-start(bf16[384,2,4,512]{3,2,1,0:T(4,128)(2,1)} %copy.27), calls=%async_computation.1 | async-start | bytes 6291456 | tf_op jit(solution)/shard_map/all_to_all | solution.py:46
  220.6 5.0 %sine_negate_fusion = (f32[1,512,512]{2,1,0:T(8,128)}, f32[1,512,512]{2,1,0:T(8,128)}) fusion(), kind=kLoop, calls=%fused_computation.53 | loop fusion | flops 3932160 | bytes 2097152 | tf_op jit(solution)/shard_map/neg | solution.py:34
  225.6 36.8 %all-to-all-done.1 = bf16[384,2,4,512]{3,2,1,0:T(4,128)(2,1)S(1)} async-done(((bf16[384,2,4,512]{3,2,1,0:T(4,128)(2,1)}), bf16[384,2,4,512]{3,2,1,0:T(4,128)(2,1)S(1)}, u32[]{:S(2)}, u32[]{:S(2)}) %all-to-all-start.1) | async-done | bytes 3145760 | tf_op jit(solution)/shard_map/all_to_all | solution.py:46
  262.4 4.9 %copy.28 = bf16[3,2,128,4,512]{4,1,3,2,0:T(2,128)(2,1)} copy(bf16[3,2,128,4,512]{4,3,1,0,2:T(4,128)(2,1)S(1)} %bitcast.102) | data formatting | bytes 6291456 | tf_op jit(solution)/shard_map/all_to_all | solution.py:46
  267.3 7.0 %copy.37 = bf16[3,2,512,512,1]{2,3,1,4,0:T(8,128)(2,1)S(1)} copy(bf16[3,2,512,512,1]{3,1,2,0,4:T(2,128)(2,1)} %bitcast.105) | data formatting | bytes 6291456 | tf_op jit(solution)/shard_map/all_to_all | solution.py:46
  274.3 6.5 %fusion.22 = f32[3,512,512,2,1]{2,1,4,3,0:T(8,128)S(1)} fusion(bf16[3,2,512,512,1]{2,3,1,4,0:T(8,128)(2,1)S(1)} %copy.37, f32[512,1,2,512]{3,0,2,1:T(8,128)} %get-tuple-element.10, f32[512,1,2,512]{3,0,2,1:T(8,128)} %get-tuple-element.5), kind=kOutput, calls=%fused_computation.28 | convolution fusion | flops 3225419776 | bytes 13631488 | tf_op jit(solution)/shard_map/xceu,zeuv->zxcv/dot_general | solution.py:58
  280.8 0.0 copy-done.5
  280.8 0.0 copy-done.6
  280.8 0.0 copy-start.3
  280.9 0.0 copy-start.4
  280.9 3.5 %fusion.28 = f32[3,512,512,2,1]{2,1,4,3,0:T(8,128)S(1)} fusion(bf16[3,2,512,512,1]{2,3,1,4,0:T(8,128)(2,1)S(1)} %copy.37, f32[512,1,2,512]{3,0,2,1:T(8,128)S(1)} %copy-done.6, f32[512,1,2,512]{3,0,2,1:T(8,128)S(1)} %copy-done.5), kind=kOutput, calls=%fused_computation.33 | convolution fusion | flops 3226468352 | bytes 13631488 | tf_op jit(solution)/shard_map/xceu,zeuv->zxcv/dot_general | solution.py:59
  284.4 12.0 %bitcast_multiply_fusion.1 = f32[3,512,512]{2,1,0:T(8,128)} fusion(f32[1,512,512]{2,1,0:T(8,128)S(1)} %copy-done.3, f32[1,512,512]{2,1,0:T(8,128)S(1)} %copy-done.4, f32[3,512,512,2,1]{2,1,4,3,0:T(8,128)S(1)} %fusion.28, f32[3,512,512,2,1]{2,1,4,3,0:T(8,128)S(1)} %fusion.22), kind=kOutput, calls=%fused_computation.18 | convolution fusion | flops 9666560000 | bytes 17825792 | tf_op jit(solution)/shard_map/zxcv,cvy->zxy/dot_general | solution.py:64
  (15 shorter events, 0.1 us)
Async XLA Ops:
  0.0 10.2 %copy-start.9 = (f32[2048]{0:T(1024)S(1)}, f32[2048]{0:T(1024)}, u32[]{:S(2)}) copy-start(f32[2048]{0:T(1024)} %param.5) | copy-start | bytes 24580
  0.0 10.3 %copy-start.7 = (f32[8,2048]{1,0:T(8,128)S(1)}, f32[8,2048]{1,0:T(8,128)}, u32[]{:S(2)}) copy-start(f32[8,2048]{1,0:T(8,128)} %param.7) | copy-start | bytes 196612
  0.0 10.3 %copy-start.8 = (s32[8,2048]{1,0:T(8,128)S(1)}, s32[8,2048]{1,0:T(8,128)}, u32[]{:S(2)}) copy-start(s32[8,2048]{1,0:T(8,128)} %param.6) | copy-start | bytes 196612
  99.5 6.1 %copy-start = (f32[3,512,512,1]{2,1,0,3:T(8,128)S(1)}, f32[3,512,512,1]{2,1,0,3:T(8,128)}, u32[]{:S(2)}) copy-start(f32[3,512,512,1]{2,1,0,3:T(8,128)} %reshape.202) | copy-start | bytes 9437188
  99.5 6.1 %copy-start.1 = (f32[512,1,512]{2,0,1:T(8,128)S(1)}, f32[512,1,512]{2,0,1:T(8,128)}, u32[]{:S(2)}) copy-start(f32[512,1,512]{2,0,1:T(8,128)} %get-tuple-element.12) | copy-start | bytes 3145732
  99.5 6.1 %copy-start.2 = (f32[512,1,512]{2,0,1:T(8,128)S(1)}, f32[512,1,512]{2,0,1:T(8,128)}, u32[]{:S(2)}) copy-start(f32[512,1,512]{2,0,1:T(8,128)} %fusion.53) | copy-start | bytes 3145732
  215.8 46.5 %all-to-all-start.1 = ((bf16[384,2,4,512]{3,2,1,0:T(4,128)(2,1)}), bf16[384,2,4,512]{3,2,1,0:T(4,128)(2,1)S(1)}, u32[]{:S(2)}, u32[]{:S(2)}) async-start(bf16[384,2,4,512]{3,2,1,0:T(4,128)(2,1)} %copy.27), calls=%async_computation.1 | async-start | bytes 6291456 | tf_op jit(solution)/shard_map/all_to_all | solution.py:46
  274.3 6.5 %copy-start.5 = (f32[512,1,2,512]{3,0,2,1:T(8,128)S(1)}, f32[512,1,2,512]{3,0,2,1:T(8,128)}, u32[]{:S(2)}) copy-start(f32[512,1,2,512]{3,0,2,1:T(8,128)} %get-tuple-element.5) | copy-start | bytes 6291460
  274.3 6.5 %copy-start.6 = (f32[512,1,2,512]{3,0,2,1:T(8,128)S(1)}, f32[512,1,2,512]{3,0,2,1:T(8,128)}, u32[]{:S(2)}) copy-start(f32[512,1,2,512]{3,0,2,1:T(8,128)} %get-tuple-element.10) | copy-start | bytes 6291460
  280.8 3.5 %copy-start.3 = (f32[1,512,512]{2,1,0:T(8,128)S(1)}, f32[1,512,512]{2,1,0:T(8,128)}, u32[]{:S(2)}) copy-start(f32[1,512,512]{2,1,0:T(8,128)} %get-tuple-element.13) | copy-start | bytes 3145732
  280.9 3.5 %copy-start.4 = (f32[1,512,512]{2,1,0:T(8,128)S(1)}, f32[1,512,512]{2,1,0:T(8,128)}, u32[]{:S(2)}) copy-start(f32[1,512,512]{2,1,0:T(8,128)} %get-tuple-element.14) | copy-start | bytes 3145732
where the time goes:
time: 301 us; the launch traced here: 297 us
  other arithmetic  108 us (36%)
  matrix products  59.6 us (20%)
  blocking collectives  53.2 us (18%)
  waiting for transfers between devices  36.8 us (12%)
  local copies, waits for them, and re-layouts  33.7 us (11%)
  starting transfers between devices  4.78 us (2%)
    scatter-add x1, other arithmetic, shards(): jnp.zeros((slab * NX * NY,), jnp.float32).at[cells.reshape(-1)]  86.7 us
    all_to_all x1, blocking collectives, shards(): lax.all_to_all(spectrum, ('zg', 'xy'), split_axis=2, concat_axis=0, tiled...  53.2 us
    all_to_all x1, waiting for transfers between devices, shards(): lax.all_to_all(mixed.reshape(depth, parts, waves, width).astype(jnp.bfloa...  36.8 us
    dot_general x1, matrix products, shards(): jnp.einsum('cuex,zxev->zcuv', forward_x, along, precision=lax.Precision.H...  22.1 us
    dot_general x1, matrix products, shards(): jnp.einsum('zxcv,cvy->zxy', middle, inverse_y, precision=lax.Precision.HI...  12 us
    all_to_all x2, local copies, waits for them, and re-layouts, shards(): lax.all_to_all(mixed.reshape(depth, parts, waves, width).astype(jnp.bfloa...  11.9 us
    dot_general x1, matrix products, shards(): jnp.einsum('zxy,yev->zxev', density, forward_y, precision=lax.Precision.H...  10.1 us
    neg x2, other arithmetic, shards(): forward_y = jnp.stack([cos_y, -sin_y], axis=1)  9.62 us
  transfers between devices with their start and end apart: 1, of which 1 were waited for; matrix products, arithmetic and copies ran while one was open for 2% of the time, Pallas kernels for 0%

commit v1 on v0

--- a/solution.py
+++ b/solution.py
@@ -39,7 +39,10 @@
     spectrum = (
         jnp.einsum("cuex,zxev->zcuv", forward_x, along, precision=lax.Precision.HIGHEST) * scale
     ).astype(jnp.bfloat16)
-    pencil = lax.all_to_all(spectrum, ("zg", "xy"), split_axis=2, concat_axis=0, tiled=True)
+    size = lax.axis_size(("zg", "xy"))
+    pieces = jnp.stack(jnp.split(spectrum, size, axis=2), axis=0)
+    pieces = lax.all_to_all(pieces, ("zg", "xy"), split_axis=0, concat_axis=0)
+    pencil = jnp.concatenate(pieces, axis=0)
     depth, parts, waves, width = pencil.shape
     blocks = pencil.reshape(depth, parts, waves, KYB, width // KYB)
     mixed = jnp.einsum("abzw,wcabj->zcabj", green, blocks, preferred_element_type=jnp.float32)

time: 301 us -> 293 us (0.973)
  local copies, waits for them, and re-layouts: 33.7 us -> 25.7 us
    convert_element_type x1 -> x0, local copies, waits for them, and re-layouts: 7.3 us -> none  [shards(): spectrum = (jnp.einsum('cuex,zxev->zcuv', forward_x, along, precision=lax...]
    another operation x0 -> x2, local copies, waits for them, and re-layouts: none -> 4.05 us  [the longest x1 4.03 us: shards(): blocks = pencil.reshape(depth, parts, waves, KYB, width // KYB)]
    reshape x1 -> x0, local copies, waits for them, and re-layouts: 4.03 us -> none  [shards(): blocks = pencil.reshape(depth, parts, waves, KYB, width // KYB)]
    all_to_all x1 -> x0, local copies, waits for them, and re-layouts: 3.28 us -> none  [shards(): lax.all_to_all(spectrum, ('zg', 'xy'), split_axis=2, concat_axis=0, tiled...]
where the time goes in v1:
time: 293 us; the launch traced here: 289 us
  other arithmetic  108 us (37%)
  matrix products  59.2 us (20%)
  blocking collectives  53.2 us (18%)
  waiting for transfers between devices  36.7 us (13%)
  local copies, waits for them, and re-layouts  25.7 us (9%)
  starting transfers between devices  4.88 us (2%)
    scatter-add x1, other arithmetic, shards(): jnp.zeros((slab * NX * NY,), jnp.float32).at[cells.reshape(-1)]  86.7 us
    all_to_all x1, blocking collectives, shards(): pieces = lax.all_to_all(pieces, ('zg', 'xy'), split_axis=0, concat_axis=0)  53.2 us
    all_to_all x1, waiting for transfers between devices, shards(): lax.all_to_all(mixed.reshape(depth, parts, waves, width).astype(jnp.bfloa...  36.7 us
    dot_general x1, matrix products, shards(): jnp.einsum('cuex,zxev->zcuv', forward_x, along, precision=lax.Precision.H...  21.6 us
    dot_general x1, matrix products, shards(): jnp.einsum('zxcv,cvy->zxy', middle, inverse_y, precision=lax.Precision.HI...  12 us
    all_to_all x2, local copies, waits for them, and re-layouts, shards(): lax.all_to_all(mixed.reshape(depth, parts, waves, width).astype(jnp.bfloa...  11.9 us
    dot_general x1, matrix products, shards(): jnp.einsum('zxy,yev->zxev', density, forward_y, precision=lax.Precision.H...  10.3 us
    neg x2, other arithmetic, shards(): forward_y = jnp.stack([cos_y, -sin_y], axis=1)  9.67 us
  transfers between devices with their start and end apart: 1, of which 1 were waited for; matrix products, arithmetic and copies ran while one was open for 2% of the time, Pallas kernels for 0%

profile of v1, /device:TPU:1, one launch (start us, length us, event | category | flops | bytes accessed | tf_op | source)
XLA Modules:
  0.0 288.9 jit_solution(14390799122390987239)
XLA Ops:
  0.0 5.0 %fusion.51 = (f32[512,1,512]{2,0,1:T(8,128)}, f32[512,1,512]{2,0,1:T(8,128)}) fusion(), kind=kLoop, calls=%fused_computation.61 | loop fusion | flops 3670016 | bytes 2097152 | tf_op jit(solution)/shard_map/sin | solution.py:17
  5.0 4.6 %fusion.53 = f32[512,1,512]{2,0,1:T(8,128)} fusion(), kind=kLoop, calls=%fused_computation.63 | loop fusion | flops 3932160 | bytes 1048576 | tf_op jit(solution)/shard_map/neg | solution.py:34
  10.3 0.0 copy-done.9
  10.3 0.0 copy-done.7
  10.3 0.0 copy-done.8
  10.4 0.1 copy.38
  10.4 0.1 compare_select_fusion
  10.5 86.7 %scatter_custom_fusion = f32[786432]{0:T(1024)S(1)} fusion(s32[16384]{0:T(1024)S(1)} %bitcast.617, f32[16384]{0:T(1024)S(1)} %bitcast.616, f32[]{:T(128)} %constant.24.clone.1), kind=kCustom, calls=%fused_computation.45 | custom fusion | flops 16384 | bytes 3145732 | tf_op jit(solution)/shard_map/scatter-add | solution.py:28
  97.2 2.3 reshape.197
  99.5 6.2 %fusion.35 = (f32[512,1,2,512]{3,0,2,1:T(8,128)}, f32[1,512,2,512]{3,1,2,0:T(8,128)S(1)}, f32[1,512,2,512]{3,1,2,0:T(8,128)S(1)}, f32[512,1,2,512]{3,0,2,1:T(8,128)}) fusion(f32[512,1,512]{2,0,1:T(8,128)} %fusion.53, f32[512,1,512]{2,0,1:T(8,128)} %get-tuple-element.12, f32[512,1,512]{2,0,1:T(8,128)} %get-tuple-element.11), kind=kLoop, calls=%fused_computation.38 | loop fusion | flops 2097152 | bytes 11534336 | tf_op jit(solution)/shard_map/stack | solution.py:56
  105.7 0.0 copy-done
  105.7 0.0 copy-done.1
  105.7 0.0 copy-done.2
  105.7 10.3 %fusion.12 = f32[3,512,2,512]{3,1,2,0:T(8,128)S(1)} fusion(f32[3,512,512,1]{2,1,0,3:T(8,128)S(1)} %copy-done, f32[512,1,512]{2,0,1:T(8,128)S(1)} %copy-done.1, f32[512,1,512]{2,0,1:T(8,128)S(1)} %copy-done.2), kind=kOutput, calls=%fused_computation.19 | convolution fusion | flops 9664200704 | bytes 11534336 | tf_op jit(solution)/shard_map/zxy,yev->zxev/dot_general | solution.py:35
  116.0 21.6 %fusion.11 = bf16[3,2,512,512]{3,2,1,0:T(8,128)(2,1)S(1)} fusion(f32[1,512,2,512]{3,1,2,0:T(8,128)S(1)} %get-tuple-element.6, f32[1,512,2,512]{3,1,2,0:T(8,128)S(1)} %get-tuple-element.9, f32[3,512,2,512]{3,1,2,0:T(8,128)S(1)} %fusion.12), kind=kOutput, calls=%fused_computation.17 | convolution fusion | flops 19331547136 | bytes 13631488 | tf_op jit(solution)/shard_map/cuex,zxev->zcuv/dot_general | solution.py:40
  140.7 53.2 %all_to_all.23 = bf16[128,3,2,4,512]{4,3,2,1,0:T(4,128)(2,1)} all-to-all(bf16[128,3,2,4,512]{4,3,2,1,0:T(4,128)(2,1)S(1)} %constant_dynamic-update-slice_fusion), channel_id=1, replica_groups=mesh['zg'=2,'xy'=64] {'zg','xy'}, dimensions={0} | all-to-all | bytes 6291456 | tf_op jit(solution)/shard_map/all_to_all | solution.py:44
  193.9 4.0 %reshape_reshape.3 = bf16[384,2,4,4,128]{4,3,2,1,0:T(4,128)(2,1)S(1)} reshape(bf16[128,3,2,4,512]{4,3,2,1,0:T(4,128)(2,1)} %all_to_all.23) | data formatting | bytes 6291456 | tf_op jit(solution)/shard_map/reshape;reshape | solution.py:47
  197.9 5.4 %convert_bitcast_fusion = bf16[384,2,4,4,128]{0,4,1,3,2:T(8,128)(2,1)S(1)} fusion(bf16[4,4,384,384]{3,2,1,0:T(8,128)(2,1)} %param.9, bf16[384,2,4,4,128]{4,3,2,1,0:T(4,128)(2,1)S(1)} %reshape_reshape.3), kind=kOutput, calls=%fused_computation.22 | convolution fusion | flops 1209532416 | bytes 11010048 | tf_op jit(solution)/shard_map/abzw,wcabj->zcabj/dot_general | solution.py:48
  203.3 0.4 copy.18
  203.7 4.4 %copy.19 = bf16[384,2,4,512]{3,2,1,0:T(4,128)(2,1)} copy(bf16[384,2,4,512]{0,3,2,1:T(8,128)(2,1)S(1)} %bitcast.612) | data formatting | bytes 6291456 | tf_op jit(solution)/shard_map/convert_element_type | solution.py:50
  208.1 4.9 %all-to-all-start.1 = ((bf16[384,2,4,512]{3,2,1,0:T(4,128)(2,1)}), bf16[384,2,4,512]{3,2,1,0:T(4,128)(2,1)S(1)}, u32[]{:S(2)}, u32[]{:S(2)}) async-start(bf16[384,2,4,512]{3,2,1,0:T(4,128)(2,1)} %copy.19), calls=%async_computation.1 | async-start | bytes 6291456 | tf_op jit(solution)/shard_map/all_to_all | solution.py:49
  213.0 5.0 %sine_negate_fusion = (f32[1,512,512]{2,1,0:T(8,128)}, f32[1,512,512]{2,1,0:T(8,128)}) fusion(), kind=kLoop, calls=%fused_computation.53 | loop fusion | flops 3932160 | bytes 2097152 | tf_op jit(solution)/shard_map/neg | solution.py:34
  218.0 36.7 %all-to-all-done.1 = bf16[384,2,4,512]{3,2,1,0:T(4,128)(2,1)S(1)} async-done(((bf16[384,2,4,512]{3,2,1,0:T(4,128)(2,1)}), bf16[384,2,4,512]{3,2,1,0:T(4,128)(2,1)S(1)}, u32[]{:S(2)}, u32[]{:S(2)}) %all-to-all-start.1) | async-done | bytes 3145760 | tf_op jit(solution)/shard_map/all_to_all | solution.py:49
  254.7 4.9 %copy.20 = bf16[3,2,128,4,512]{4,1,3,2,0:T(2,128)(2,1)} copy(bf16[3,2,128,4,512]{4,3,1,0,2:T(4,128)(2,1)S(1)} %bitcast.611) | data formatting | bytes 6291456 | tf_op jit(solution)/shard_map/all_to_all | solution.py:49
  259.6 7.0 %copy.28 = bf16[3,2,512,512,1]{2,3,1,4,0:T(8,128)(2,1)S(1)} copy(bf16[3,2,512,512,1]{3,1,2,0,4:T(2,128)(2,1)} %bitcast.613) | data formatting | bytes 6291456 | tf_op jit(solution)/shard_map/all_to_all | solution.py:49
  266.6 0.0 copy-start.5
  266.7 0.0 copy-start.6
  266.7 6.5 %fusion.22 = f32[3,512,512,2,1]{2,1,4,3,0:T(8,128)S(1)} fusion(bf16[3,2,512,512,1]{2,3,1,4,0:T(8,128)(2,1)S(1)} %copy.28, f32[512,1,2,512]{3,0,2,1:T(8,128)} %get-tuple-element.10, f32[512,1,2,512]{3,0,2,1:T(8,128)} %get-tuple-element.5), kind=kOutput, calls=%fused_computation.28 | convolution fusion | flops 3225419776 | bytes 13631488 | tf_op jit(solution)/shard_map/xceu,zeuv->zxcv/dot_general | solution.py:61
  273.2 0.0 copy-done.5
  273.2 0.0 copy-done.6
  273.2 3.5 %fusion.28 = f32[3,512,512,2,1]{2,1,4,3,0:T(8,128)S(1)} fusion(bf16[3,2,512,512,1]{2,3,1,4,0:T(8,128)(2,1)S(1)} %copy.28, f32[512,1,2,512]{3,0,2,1:T(8,128)S(1)} %copy-done.6, f32[512,1,2,512]{3,0,2,1:T(8,128)S(1)} %copy-done.5), kind=kOutput, calls=%fused_computation.33 | convolution fusion | flops 3226468352 | bytes 13631488 | tf_op jit(solution)/shard_map/xceu,zeuv->zxcv/dot_general | solution.py:62
  276.7 12.0 %bitcast_multiply_fusion.1 = f32[3,512,512]{2,1,0:T(8,128)} fusion(f32[1,512,512]{2,1,0:T(8,128)S(1)} %copy-done.3, f32[1,512,512]{2,1,0:T(8,128)S(1)} %copy-done.4, f32[3,512,512,2,1]{2,1,4,3,0:T(8,128)S(1)} %fusion.28, f32[3,512,512,2,1]{2,1,4,3,0:T(8,128)S(1)} %fusion.22), kind=kOutput, calls=%fused_computation.18 | convolution fusion | flops 9666560000 | bytes 17825792 | tf_op jit(solution)/shard_map/zxcv,cvy->zxy/dot_general | solution.py:67
  (141 shorter events, 2.7 us)
Async XLA Ops:
  0.0 10.3 %copy-start.9 = (f32[2048]{0:T(1024)S(1)}, f32[2048]{0:T(1024)}, u32[]{:S(2)}) copy-start(f32[2048]{0:T(1024)} %param.5) | copy-start | bytes 24580
  0.0 10.3 %copy-start.7 = (f32[8,2048]{1,0:T(8,128)S(1)}, f32[8,2048]{1,0:T(8,128)}, u32[]{:S(2)}) copy-start(f32[8,2048]{1,0:T(8,128)} %param.7) | copy-start | bytes 196612
  0.0 10.3 %copy-start.8 = (s32[8,2048]{1,0:T(8,128)S(1)}, s32[8,2048]{1,0:T(8,128)}, u32[]{:S(2)}) copy-start(s32[8,2048]{1,0:T(8,128)} %param.6) | copy-start | bytes 196612
  99.5 6.2 %copy-start = (f32[3,512,512,1]{2,1,0,3:T(8,128)S(1)}, f32[3,512,512,1]{2,1,0,3:T(8,128)}, u32[]{:S(2)}) copy-start(f32[3,512,512,1]{2,1,0,3:T(8,128)} %reshape.197) | copy-start | bytes 9437188
  99.5 6.2 %copy-start.1 = (f32[512,1,512]{2,0,1:T(8,128)S(1)}, f32[512,1,512]{2,0,1:T(8,128)}, u32[]{:S(2)}) copy-start(f32[512,1,512]{2,0,1:T(8,128)} %get-tuple-element.12) | copy-start | bytes 3145732
  99.5 6.2 %copy-start.2 = (f32[512,1,512]{2,0,1:T(8,128)S(1)}, f32[512,1,512]{2,0,1:T(8,128)}, u32[]{:S(2)}) copy-start(f32[512,1,512]{2,0,1:T(8,128)} %fusion.53) | copy-start | bytes 3145732
  208.1 46.6 %all-to-all-start.1 = ((bf16[384,2,4,512]{3,2,1,0:T(4,128)(2,1)}), bf16[384,2,4,512]{3,2,1,0:T(4,128)(2,1)S(1)}, u32[]{:S(2)}, u32[]{:S(2)}) async-start(bf16[384,2,4,512]{3,2,1,0:T(4,128)(2,1)} %copy.19), calls=%async_computation.1 | async-start | bytes 6291456 | tf_op jit(solution)/shard_map/all_to_all | solution.py:49
  266.6 6.5 %copy-start.5 = (f32[512,1,2,512]{3,0,2,1:T(8,128)S(1)}, f32[512,1,2,512]{3,0,2,1:T(8,128)}, u32[]{:S(2)}) copy-start(f32[512,1,2,512]{3,0,2,1:T(8,128)} %get-tuple-element.5) | copy-start | bytes 6291460
  266.7 6.5 %copy-start.6 = (f32[512,1,2,512]{3,0,2,1:T(8,128)S(1)}, f32[512,1,2,512]{3,0,2,1:T(8,128)}, u32[]{:S(2)}) copy-start(f32[512,1,2,512]{3,0,2,1:T(8,128)} %get-tuple-element.10) | copy-start | bytes 6291460
  273.2 3.5 %copy-start.3 = (f32[1,512,512]{2,1,0:T(8,128)S(1)}, f32[1,512,512]{2,1,0:T(8,128)}, u32[]{:S(2)}) copy-start(f32[1,512,512]{2,1,0:T(8,128)} %get-tuple-element.13) | copy-start | bytes 3145732
  273.2 3.5 %copy-start.4 = (f32[1,512,512]{2,1,0:T(8,128)S(1)}, f32[1,512,512]{2,1,0:T(8,128)}, u32[]{:S(2)}) copy-start(f32[1,512,512]{2,1,0:T(8,128)} %get-tuple-element.14) | copy-start | bytes 3145732
